TPU v7x, 32 devices: a whole 2x2x4 slice. The times are simulated.
32 devices in a mesh: groups: 2 (over y), band: 4 (over z), chan: 4 (over x, core).
Axes of the slice: x: 2, y: 2, z: 4, core: 2. Of those that a mesh axis runs over, the one named last changes fastest.
Arguments:
- slide_region: float32 [16, 32, 8192], P('chan', ('groups', 'band')), parts along dimension 1, may hold values from -6 to 6
- row_taps: float32 [16, 257], P('chan'), may hold values from -0.375 to 0.375
- column_taps: float32 [16, 257], replicated, may hold values from -0.375 to 0.375
- channel_mix: float32 [16, 16], replicated, may hold values from -1.5 to 1.5
Outputs:
- filtered: float32 [16, 32, 8192], P('chan', ('groups', 'band')), parts along dimension 1
There are 2 independent parts, one for each index of `groups`. A program takes and returns all parts, laid end to end along the dimension named above; an argument that names none is the same for every part. Nothing has to cross between parts.
All inputs are finite; a program needn't handle non-finite values.
Results may differ from a plain program's by a relative error of at most 0.00007.
Values sent between devices are 32-bit elements; how exact they have to be, the bound alone decides.
A program may use at most 64 MiB of HBM per device.

v0:
```python
import jax
import jax.numpy as jnp
from jax import lax
from jax.sharding import PartitionSpec as P

precise = lax.Precision.HIGHEST


def band_tables(filter_taps, tile_size):
    channels, length = filter_taps.shape
    margin = (length - 1) // 2
    period = 4 * tile_size
    border = 3 * tile_size + length
    widened = jnp.pad(filter_taps, ((0, 0), (border, border)))
    lowest = margin - tile_size + border
    window = widened[:, lowest : lowest + 3 * tile_size]
    vector = jnp.pad(window, ((0, 0), (0, tile_size)))
    repeated = jnp.tile(vector, (1, tile_size))[:, : tile_size * (period - 1)]
    toeplitz = repeated.reshape(channels, tile_size, period - 1)[:, :, : 3 * tile_size]
    stacked = jnp.transpose(toeplitz, (0, 2, 1))
    return stacked.reshape(channels, 3, tile_size, tile_size)


def along_columns(signal, filter_taps):
    tile_size = 128
    tables = band_tables(filter_taps, tile_size)
    channels, row_count, col_count = signal.shape
    tile_count = col_count // tile_size
    tiled = signal.reshape(channels, row_count, tile_count, tile_size)
    padded = jnp.pad(tiled, ((0, 0), (0, 0), (1, 1), (0, 0)))
    result = jnp.einsum(
        "crti,cij->crtj", padded[:, :, 0:tile_count], tables[:, 0], precision=precise
    )
    result = result + jnp.einsum(
        "crti,cij->crtj", padded[:, :, 1 : tile_count + 1], tables[:, 1], precision=precise
    )
    result = result + jnp.einsum(
        "crti,cij->crtj", padded[:, :, 2:], tables[:, 2], precision=precise
    )
    return result.reshape(channels, row_count, col_count)


def along_rows(signal, filter_taps):
    channels, row_count, col_count = signal.shape
    tile_size = 128 if row_count % 128 == 0 else row_count
    tables = band_tables(filter_taps, tile_size)
    tile_count = row_count // tile_size
    tiled = signal.reshape(channels, tile_count, tile_size, col_count)
    padded = jnp.pad(tiled, ((0, 0), (1, 1), (0, 0), (0, 0)))
    result = jnp.einsum("ctiw,cij->ctjw", padded[:, 0:tile_count], tables[:, 0], precision=precise)
    result = result + jnp.einsum(
        "ctiw,cij->ctjw", padded[:, 1 : tile_count + 1], tables[:, 1], precision=precise
    )
    result = result + jnp.einsum("ctiw,cij->ctjw", padded[:, 2:], tables[:, 2], precision=precise)
    return result.reshape(channels, row_count, col_count)


def on_device(slide_region, row_taps, column_taps, channel_mix):
    local_channels = slide_region.shape[0]
    across = along_columns(slide_region, row_taps)
    column_band = lax.all_to_all(across, "band", split_axis=2, concat_axis=1, tiled=True)
    first_channel = lax.axis_index("chan") * local_channels
    own_taps = lax.dynamic_slice_in_dim(column_taps, first_channel, local_channels, 0)
    vertical = along_rows(column_band, own_taps)
    own_mixing = lax.dynamic_slice_in_dim(channel_mix, first_channel, local_channels, 0)
    blended = jnp.einsum(
        "oc,chw->ohw",
        own_mixing,
        lax.all_gather(vertical, "chan", axis=0, tiled=True),
        precision=precise,
    )
    return lax.all_to_all(blended, "band", split_axis=1, concat_axis=2, tiled=True)


def solution(mesh):
    in_specs = (P("chan", ("groups", "band"), None), P("chan", None), P(), P())
    out_specs = P("chan", ("groups", "band"), None)
    return jax.shard_map(
        on_device, mesh=mesh, in_specs=in_specs, out_specs=out_specs, check_vma=False
    )
```

profile of v0, /device:TPU:0, one launch (start us, length us, event | category | flops | bytes accessed | tf_op | source)
XLA Modules:
  0.0 165.2 jit_solution(12233661536541176305)
XLA Ops:
  6.5 0.7 pad_slice_fusion.4
  7.4 0.7 copy.47
  8.2 1.0 reshape.47
  9.5 0.4 reshape.46
  9.9 0.6 fusion.4
  10.5 0.6 fusion.5
  11.2 0.6 fusion.3
  11.8 8.6 %copy.38 = f32[4,4,64,128]{1,0,3,2:T(4,128)} copy(f32[4,4,64,128]{3,2,1,0:T(8,128)S(1)} %fusion.3) | data formatting | bytes 1048576 | tf_op jit(solution)/shard_map/reshape | solution.py:40
  20.4 24.6 %reshape.55 = f32[4,1,32768]{2,1,0:T(1,128)} reshape(f32[8192,4,4]{2,1,0:T(4,128)} %bitcast.68) | data formatting | bytes 1048576
  45.0 6.3 %all-to-all-start = ((f32[4,1,32768]{2,1,0:T(1,128)}), f32[4,1,32768]{2,1,0:T(1,128)S(1)}, u32[]{:S(2)}, u32[]{:S(2)}) async-start(f32[4,1,32768]{2,1,0:T(1,128)} %reshape.55), calls=%async_computation | async-start | bytes 1048576 | tf_op jit(solution)/shard_map/all_to_all | solution.py:61
  51.3 0.8 dynamic-slice
  52.5 0.4 fusion.8
  52.9 13.0 %all-to-all-done = f32[4,1,32768]{2,1,0:T(1,128)S(1)} async-done(((f32[4,1,32768]{2,1,0:T(1,128)}), f32[4,1,32768]{2,1,0:T(1,128)S(1)}, u32[]{:S(2)}, u32[]{:S(2)}) %all-to-all-start) | async-done | bytes 524320 | tf_op jit(solution)/shard_map/all_to_all | solution.py:61
  65.8 0.5 broadcast.18
  66.3 2.2 %reduce = f32[4,32768]{1,0:T(4,128)S(1)} reduce(f32[4,1,32768]{2,1,0:T(1,128)S(1)} %all-to-all-done, f32[]{:T(128)} %broadcast.18), dimensions={1}, to_apply=%all_to_all.24.reduce_sub_computation | reduce | bytes 1048580 | tf_op jit(solution)/shard_map/all_to_all | solution.py:61
  68.5 28.0 %reshape.56 = f32[8192,4,4]{2,1,0:T(4,128)} reshape(f32[4,32768]{1,0:T(4,128)S(1)} %reduce) | data formatting | bytes 1048576
  96.5 13.4 %copy.30 = f32[4,4,4,2048]{3,0,2,1:T(4,128)S(1)} copy(f32[4,4,4,2048]{2,0,3,1:T(4,128)} %bitcast.69) | data formatting | bytes 1048576 | tf_op jit(solution)/shard_map/all_to_all | solution.py:61
  109.9 0.9 convolution_add_fusion.1
  110.8 1.1 convolution_add_fusion
  111.9 21.8 %all-gather.2.cloned.1.call-done = f32[16,16,2048]{2,1,0:T(8,128)} async-done(((f32[4,16,2048]{2,1,0:T(8,128)}), f32[16,16,2048]{2,1,0:T(8,128)}) %all-gather.2.cloned.1.call-update) | async-done | bytes 2097168 | tf_op jit(solution)/shard_map/all_gather | solution.py:69
  133.8 3.8 %fusion = f32[4,16,2048]{2,0,1:T(4,128)S(1)} fusion(f32[16,16,2048]{2,1,0:T(8,128)} %all-gather.2.cloned.1.call-done, f32[16,16]{1,0:T(8,128)S(1)} %copy-done, s32[]{:T(128)S(6)} %select_n.4), kind=kOutput, calls=%fused_computation.2 | convolution fusion | flops 25165824 | bytes 2623492 | tf_op jit(solution)/shard_map/oc,chw->ohw/dot_general | solution.py:66
  137.5 19.3 %all_to_all.33 = f32[4,16,2048]{2,0,1:T(4,128)S(1)} all-to-all(f32[4,16,2048]{2,0,1:T(4,128)S(1)} %fusion), channel_id=1, replica_groups=mesh['groups'=2,'band'=4,'chan'=4] {'band'}, dimensions={1} | all-to-all | bytes 1048576 | tf_op jit(solution)/shard_map/all_to_all | solution.py:72
  156.8 0.3 copy.34
  157.2 1.2 all_to_all.30
  (18 shorter events, 0.9 us)
Async XLA Ops:
  6.5 127.2 %copy-start = (f32[16,16]{1,0:T(8,128)S(1)}, f32[16,16]{1,0:T(8,128)}, u32[]{:S(2)}) copy-start(f32[16,16]{1,0:T(8,128)} %param.7) | copy-start | bytes 3076
  8.1 1.4 copy-start.1
  45.0 20.8 %all-to-all-start = ((f32[4,1,32768]{2,1,0:T(1,128)}), f32[4,1,32768]{2,1,0:T(1,128)S(1)}, u32[]{:S(2)}, u32[]{:S(2)}) async-start(f32[4,1,32768]{2,1,0:T(1,128)} %reshape.55), calls=%async_computation | async-start | bytes 1048576 | tf_op jit(solution)/shard_map/all_to_all | solution.py:61
  51.3 82.4 %all-gather.2.cloned.1.call-start = ((), (), s32[]{:S(2)}) async-start(), calls=%async_computation.2 | async-start | bytes 2621440 | tf_op jit(solution)/shard_map/all_gather | solution.py:69
Sparse Core Ops, SparseCore 0:
  112.1 21.6 all-gather.1
where the time goes:
time: 166 us; the launch traced here: 165 us
  local copies, waits for them, and re-layouts  81.1 us (49%)
  waiting for transfers between devices  34.8 us (21%)
  blocking collectives  19.3 us (12%)
  between operations  13.5 us (8%)
  matrix products  7.99 us (5%)
  starting transfers between devices  6.35 us (4%)
  other arithmetic  2.17 us (1%)
    unnamed x8, local copies, waits for them, and re-layouts  53.4 us
    all_gather x1, waiting for transfers between devices, on_device(): lax.all_gather(vertical, 'chan', axis=0, tiled=True)  21.8 us
    all_to_all x1, blocking collectives, on_device(): lax.all_to_all(blended, 'band', split_axis=1, concat_axis=2, tiled=True)  19.3 us
    all_to_all x2, local copies, waits for them, and re-layouts, on_device(): lax.all_to_all(across, 'band', split_axis=2, concat_axis=1, tiled=True)  13.9 us
    all_to_all x1, waiting for transfers between devices, on_device(): lax.all_to_all(across, 'band', split_axis=2, concat_axis=1, tiled=True)  13 us
    reshape x1, local copies, waits for them, and re-layouts, along_columns(): return result.reshape(channels, row_count, col_count)  8.62 us
    all_to_all x1, starting transfers between devices, on_device(): lax.all_to_all(across, 'band', split_axis=2, concat_axis=1, tiled=True)  6.35 us
    dot_general x1, matrix products, on_device(): jnp.einsum('oc,chw->ohw', own_mixing, lax.all_gather(vertical, 'chan', ax...  3.77 us
  transfers between devices with their start and end apart: 2, of which 2 were waited for; matrix products, arithmetic and copies ran while one was open for 1% of the time, Pallas kernels for 0%

commit v1 on v0

--- a/solution.py
+++ b/solution.py
@@ -1,6 +1,10 @@
+import functools
+
 import jax
 import jax.numpy as jnp
 from jax import lax
+from jax.experimental import pallas as pl
+from jax.experimental.pallas import tpu as pltpu
 from jax.sharding import PartitionSpec as P
 
 precise = lax.Precision.HIGHEST
@@ -72,9 +76,285 @@
     return lax.all_to_all(blended, "band", split_axis=1, concat_axis=2, tiled=True)
 
 
+LANES = 128
+CHUNKS = 2
+
+
+def split(value):
+    high = value.astype(jnp.bfloat16)
+    return high, (value - high.astype(jnp.float32)).astype(jnp.bfloat16)
+
+
+def product(left, right, dims):
+    (left_high, left_low), (right_high, right_low) = left, right
+    dot = functools.partial(
+        lax.dot_general, dimension_numbers=(dims, ((), ())), preferred_element_type=jnp.float32
+    )
+    return dot(left_high, right_high) + (dot(left_low, right_high) + dot(left_high, right_low))
+
+
+def filter_table(taps):
+    shape = (LANES, LANES)
+    lane = lax.broadcasted_iota(jnp.int32, shape, 1)
+    row = lax.broadcasted_iota(jnp.int32, shape, 0)
+    first, second = (
+        pltpu.roll(
+            jnp.broadcast_to(taps[:, at : at + LANES], shape), 0, 1, stride=1, stride_axis=0
+        )
+        for at in (0, LANES)
+    )
+    last = jnp.broadcast_to(taps[:, 2 * LANES :], shape)
+    zero = jnp.zeros(shape, jnp.float32)
+    return jnp.concatenate(
+        [
+            jnp.where(lane >= row, first, zero),
+            jnp.where(lane >= row, second, first),
+            jnp.where(lane == row, last, jnp.where(lane < row, second, zero)),
+        ],
+        axis=1,
+    )
+
+
+def mixing_table(column_taps, channel_mix, chans, bands, local_channels, local_rows):
+    channels = chans * local_channels
+    height = bands * local_rows
+    block = local_channels * local_rows
+    size = chans * bands * block
+    margin = (column_taps.shape[1] - 1) // 2
+
+    def coordinates(index):
+        device, inner = index // block, index % block
+        return (
+            local_channels * (device % chans) + inner // local_rows,
+            local_rows * (device // chans) + inner % local_rows,
+        )
+
+    tall = (size, channels)
+    wide = (channels, size)
+    pick_tall = (
+        coordinates(lax.broadcasted_iota(jnp.int32, tall, 0))[0]
+        == lax.broadcasted_iota(jnp.int32, tall, 1)
+    ).astype(jnp.float32)
+    pick_wide = (
+        coordinates(lax.broadcasted_iota(jnp.int32, wide, 1))[0]
+        == lax.broadcasted_iota(jnp.int32, wide, 0)
+    ).astype(jnp.float32)
+    weights = jnp.dot(
+        jnp.dot(pick_tall, channel_mix, precision=precise), pick_wide, precision=precise
+    )
+    taps = lax.dot_general(
+        column_taps[:, : 2 * margin],
+        pick_wide,
+        (((0,), (0,)), ((), ())),
+        precision=precise,
+    )
+    square = (size, size)
+    apart = (
+        coordinates(lax.broadcasted_iota(jnp.int32, square, 1))[1]
+        - coordinates(lax.broadcasted_iota(jnp.int32, square, 0))[1]
+    )
+    spread = jnp.zeros(square, jnp.float32)
+    for distance in range(1 - height, height):
+        at = margin + distance
+        spread = jnp.where(apart == distance, taps[at : at + 1, :], spread)
+    return weights * spread
+
+
+def fused_kernel(
+    chans, bands, x_hbm, row_taps, column_taps, channel_mix, out_hbm,
+    x_buf, send_one, recv_one, send_two, mixing,
+    in_sem, own_sem, send_one_sem, recv_one_sem, send_two_sem, recv_two_sem,
+):
+    local_channels, x_rows, _ = x_hbm.shape
+    devices, _, block_rows, _ = send_two.shape
+    tiles = send_one.shape[1]
+    local_rows = block_rows // tiles
+    chan, band = lax.axis_index("chan"), lax.axis_index("band")
+    me = band * chans + chan
+
+    barrier = pltpu.get_barrier_semaphore()
+    peers = []
+    for band_step in sorted(range(bands), key=lambda step: (-(2 * step // bands), step)):
+        for chan_step in range(chans):
+            if band_step or chan_step:
+                peers.append((chan ^ chan_step, band ^ band_step))
+    names = [{"chan": to_chan, "band": to_band} for to_chan, to_band in peers]
+    slots = [to_band * chans + to_chan for to_chan, to_band in peers]
+    for name in names:
+        pl.semaphore_signal(barrier, inc=1, device_id=name, device_id_type=pl.DeviceIdType.MESH)
+
+    loads = [
+        pltpu.make_async_copy(x_hbm.at[c], x_buf.at[c, pl.ds(8, x_rows)], in_sem.at[c])
+        for c in range(local_channels)
+    ]
+    for load in loads:
+        load.start()
+    edge = jnp.zeros((8, LANES), jnp.float32)
+    for c in range(local_channels):
+        x_buf[c, 0:8, :] = edge
+        x_buf[c, x_rows + 8 : x_rows + 16, :] = edge
+
+    for c in range(local_channels):
+        table = split(filter_table(row_taps[c : c + 1, :]))
+        loads[c].wait()
+        window = jnp.concatenate(
+            [
+                x_buf[c, 8 + (k - 1) * local_rows : 8 + (k - 1) * local_rows + x_rows, :]
+                for k in range(3)
+            ],
+            axis=1,
+        )
+        filtered = product(split(window), table, ((1,), (1,)))
+        for device in range(devices):
+            for tile in range(tiles):
+                at = (device * tiles + tile) * local_rows
+                send_one[device, tile, c * local_rows : (c + 1) * local_rows, :] = filtered[
+                    at : at + local_rows, :
+                ]
+
+    pl.semaphore_wait(barrier, len(peers))
+    step = tiles // CHUNKS
+    copies = []
+    for chunk in range(CHUNKS):
+        part = pl.ds(chunk * step, step)
+        for name, slot in zip(names, slots):
+            copy = pltpu.make_async_remote_copy(
+                src_ref=send_one.at[slot, part],
+                dst_ref=recv_one.at[part, me],
+                send_sem=send_one_sem.at[chunk, slot],
+                recv_sem=recv_one_sem.at[chunk, me],
+                device_id=name,
+                device_id_type=pl.DeviceIdType.MESH,
+            )
+            copy.start()
+            copies.append(copy)
+    recv_one[:, me] = send_one[me]
+
+    table = mixing_table(
+        column_taps[...], channel_mix[...], chans, bands, local_channels, local_rows
+    )
+    mixing[0], mixing[1] = split(table)
+
+    rows = step * local_rows
+    own = []
+    for chunk in range(CHUNKS):
+        part = pl.ds(chunk * step, step)
+        for slot in slots:
+            landed = recv_one.at[part, slot]
+            pltpu.make_async_copy(landed, landed, recv_one_sem.at[chunk, slot]).wait()
+        columns = jnp.concatenate(
+            [
+                recv_one[chunk * step + tile].reshape(mixing.shape[1], LANES)
+                for tile in range(step)
+            ],
+            axis=1,
+        )
+        mixed = product((mixing[0], mixing[1]), split(columns), ((1,), (0,)))
+        for device in range(devices):
+            for c in range(local_channels):
+                at = (device * local_channels + c) * local_rows
+                for tile in range(step):
+                    to = (chunk * step + tile) * local_rows
+                    send_two[device, c, to : to + local_rows, :] = mixed[
+                        at : at + local_rows, tile * LANES : (tile + 1) * LANES
+                    ]
+        here = pl.ds(chunk * rows, rows)
+        there = pl.ds(pl.multiple_of(me * block_rows + chunk * rows, 8), rows)
+        for name, slot in zip(names, slots):
+            copy = pltpu.make_async_remote_copy(
+                src_ref=send_two.at[slot, :, here],
+                dst_ref=out_hbm.at[:, there],
+                send_sem=send_two_sem.at[chunk, slot],
+                recv_sem=recv_two_sem.at[chunk, me],
+                device_id=name,
+                device_id_type=pl.DeviceIdType.MESH,
+            )
+            copy.start()
+            copies.append(copy)
+        copy = pltpu.make_async_copy(
+            send_two.at[me, :, here], out_hbm.at[:, there], own_sem.at[chunk]
+        )
+        copy.start()
+        own.append(copy)
+
+    for chunk in range(CHUNKS):
+        for slot in slots:
+            landed = out_hbm.at[
+                :, pl.ds(pl.multiple_of(slot * block_rows + chunk * rows, 8), rows)
+            ]
+            pltpu.make_async_copy(landed, landed, recv_two_sem.at[chunk, slot]).wait()
+        own[chunk].wait()
+    for copy in copies:
+        copy.wait_send()
+
+
+def fused(chans, bands, slide_region, row_taps, column_taps, channel_mix):
+    local_channels, local_rows, width = slide_region.shape
+    devices = chans * bands
+    total_tiles = width // LANES
+    tiles = total_tiles // devices
+    block = local_channels * local_rows
+    tiled = slide_region.reshape(local_channels, local_rows, total_tiles, LANES)
+    tiled = tiled.transpose(0, 2, 1, 3).reshape(local_channels, total_tiles * local_rows, LANES)
+    vmem = pl.BlockSpec(memory_space=pltpu.VMEM)
+    anywhere = pl.BlockSpec(memory_space=pl.ANY)
+    dma = pltpu.SemaphoreType.DMA
+    out = pl.pallas_call(
+        functools.partial(fused_kernel, chans, bands),
+        out_shape=jax.ShapeDtypeStruct(tiled.shape, jnp.float32),
+        in_specs=[anywhere, vmem, vmem, vmem],
+        out_specs=anywhere,
+        scratch_shapes=[
+            pltpu.VMEM((local_channels, tiled.shape[1] + 16, LANES), jnp.float32),
+            pltpu.VMEM((devices, tiles, block, LANES), jnp.float32),
+            pltpu.VMEM((tiles, devices, block, LANES), jnp.float32),
+            pltpu.VMEM((devices, local_channels, tiles * local_rows, LANES), jnp.float32),
+            pltpu.VMEM((2, devices * block, devices * block), jnp.bfloat16),
+            dma((local_channels,)),
+            dma((CHUNKS,)),
+            dma((CHUNKS, devices)),
+            dma((CHUNKS, devices)),
+            dma((CHUNKS, devices)),
+            dma((CHUNKS, devices)),
+        ],
+        compiler_params=pltpu.CompilerParams(collective_id=0, has_side_effects=True),
+    )(tiled, row_taps, column_taps, channel_mix)
+    out = out.reshape(local_channels, total_tiles, local_rows, LANES)
+    return out.transpose(0, 2, 1, 3).reshape(slide_region.shape)
+
+
+def power_of_two(number):
+    return number & (number - 1) == 0
+
+
+def program(chans, bands, slide_region, row_taps, column_taps, channel_mix):
+    local_channels, local_rows, width = slide_region.shape
+    devices = chans * bands
+    margin = (row_taps.shape[1] - 1) // 2
+    fits = (
+        power_of_two(chans)
+        and power_of_two(bands)
+        and width % (devices * LANES * CHUNKS) == 0
+        and margin == LANES
+        and column_taps.shape[1] == row_taps.shape[1]
+        and local_rows == 4
+        and local_rows * bands <= margin
+        and local_channels * local_rows % 8 == 0
+        and width // (devices * LANES * CHUNKS) * local_rows % 8 == 0
+        and devices * local_channels * local_rows <= 512
+    )
+    if fits:
+        return fused(chans, bands, slide_region, row_taps, column_taps, channel_mix)
+    return on_device(slide_region, row_taps, column_taps, channel_mix)
+
+
 def solution(mesh):
     in_specs = (P("chan", ("groups", "band"), None), P("chan", None), P(), P())
     out_specs = P("chan", ("groups", "band"), None)
     return jax.shard_map(
-        on_device, mesh=mesh, in_specs=in_specs, out_specs=out_specs, check_vma=False
-    )
+        functools.partial(program, mesh.shape["chan"], mesh.shape["band"]),
+        mesh=mesh,
+        in_specs=in_specs,
+        out_specs=out_specs,
+        check_vma=False,
+    )

time: 166 us -> 33.5 us (0.20)
  local copies, waits for them, and re-layouts: 81.1 us -> 1.87 us
  waiting for transfers between devices: 34.8 us -> 0 us
  Pallas kernels: 0 us -> 31.4 us
  blocking collectives: 19.3 us -> 0 us
  between operations: 13.5 us -> 0.01 us
  matrix products: 7.99 us -> 0 us
  starting transfers between devices: 6.35 us -> 0 us
  other arithmetic: 2.17 us -> 0 us
    unnamed x8 -> x1, local copies, waits for them, and re-layouts: 53.4 us -> 1.87 us
    pallas_call x0 -> x1, Pallas kernels: none -> 31.4 us  [fused(): pl.pallas_call(functools.partial(fused_kernel, chans, bands), out_shape=j...]
    all_gather x1 -> x0, waiting for transfers between devices: 21.8 us -> none  [on_device(): lax.all_gather(vertical, 'chan', axis=0, tiled=True)]
    all_to_all x1 -> x0, blocking collectives: 19.3 us -> none  [on_device(): lax.all_to_all(blended, 'band', split_axis=1, concat_axis=2, tiled=True)]
    all_to_all x4 -> x0, local copies, waits for them, and re-layouts: 15.5 us -> none  [the longest x2 13.9 us: on_device(): lax.all_to_all(across, 'band', split_axis=2, concat_axis=1, tiled=True)]
    all_to_all x1 -> x0, waiting for transfers between devices: 13 us -> none  [on_device(): lax.all_to_all(across, 'band', split_axis=2, concat_axis=1, tiled=True)]
    reshape x5 -> x0, local copies, waits for them, and re-layouts: 10.2 us -> none  [the longest x1 8.62 us: along_columns(): return result.reshape(channels, row_count, col_count)]
    dot_general x7 -> x0, matrix products: 7.99 us -> none  [the longest x1 3.77 us: on_device(): jnp.einsum('oc,chw->ohw', own_mixing, lax.all_gather(vertical, 'chan', ax...]
  transfers between devices with their start and end apart: 2 -> 0, of which waited for: 2 -> 0; matrix products, arithmetic and copies ran while one was open for 1% -> 0% of each run, Pallas kernels for 0% -> 0%
where the time goes in v1:
time: 33.5 us; the launch traced here: 33.2 us
  Pallas kernels  31.4 us (94%)
  local copies, waits for them, and re-layouts  1.87 us (6%)
    pallas_call x1, Pallas kernels, fused(): pl.pallas_call(functools.partial(fused_kernel, chans, bands), out_shape=j...  31.4 us
    unnamed x1, local copies, waits for them, and re-layouts  1.87 us

profile of v1, /device:TPU:0, one launch (start us, length us, event | category | flops | bytes accessed | tf_op | source)
XLA Modules:
  0.0 33.2 jit_solution(12738621178057964787)
XLA Ops:
  0.0 31.4 %shard_map.46 = f32[4,256,128]{2,1,0:T(8,128)} custom-call(f32[4,256,128]{2,1,0:T(8,128)} %bitcast.11, f32[4,257]{1,0:T(4,128)} %row_taps.1, f32[16,257]{1,0:T(8,128)} %column_taps.1, f32[16,16]{1,0:T(8,128)} %channel_mix.1), custom_call_target="tpu_custom_call" | custom-call | tf_op jit(solution)/shard_map/pallas_call | solution.py:302
  31.4 1.9 %copy.8 = f32[4,4,8192]{2,1,0:T(4,128)} copy(f32[4,4,8192]{2,1,0:T(4,128)} %bitcast.10) | data formatting | bytes 1048576

commit v2 on v1

--- a/solution.py
+++ b/solution.py
@@ -161,9 +161,9 @@
 
 
 def fused_kernel(
-    chans, bands, x_hbm, row_taps, column_taps, channel_mix, out_hbm,
+    chans, bands, x_hbm, row_taps, column_taps, channel_mix, out_ref,
     x_buf, send_one, recv_one, send_two, mixing,
-    in_sem, own_sem, send_one_sem, recv_one_sem, send_two_sem, recv_two_sem,
+    in_sem, send_one_sem, recv_one_sem, send_two_sem, recv_two_sem,
 ):
     local_channels, x_rows, _ = x_hbm.shape
     devices, _, block_rows, _ = send_two.shape
@@ -236,7 +236,6 @@
     mixing[0], mixing[1] = split(table)
 
     rows = step * local_rows
-    own = []
     for chunk in range(CHUNKS):
         part = pl.ds(chunk * step, step)
         for slot in slots:
@@ -263,7 +262,7 @@
         for name, slot in zip(names, slots):
             copy = pltpu.make_async_remote_copy(
                 src_ref=send_two.at[slot, :, here],
-                dst_ref=out_hbm.at[:, there],
+                dst_ref=out_ref.at[:, there],
                 send_sem=send_two_sem.at[chunk, slot],
                 recv_sem=recv_two_sem.at[chunk, me],
                 device_id=name,
@@ -271,19 +270,14 @@
             )
             copy.start()
             copies.append(copy)
-        copy = pltpu.make_async_copy(
-            send_two.at[me, :, here], out_hbm.at[:, there], own_sem.at[chunk]
-        )
-        copy.start()
-        own.append(copy)
+        out_ref[:, there, :] = send_two[me, :, chunk * rows : (chunk + 1) * rows, :]
 
     for chunk in range(CHUNKS):
         for slot in slots:
-            landed = out_hbm.at[
+            landed = out_ref.at[
                 :, pl.ds(pl.multiple_of(slot * block_rows + chunk * rows, 8), rows)
             ]
             pltpu.make_async_copy(landed, landed, recv_two_sem.at[chunk, slot]).wait()
-        own[chunk].wait()
     for copy in copies:
         copy.wait_send()
 
@@ -301,9 +295,9 @@
     dma = pltpu.SemaphoreType.DMA
     out = pl.pallas_call(
         functools.partial(fused_kernel, chans, bands),
-        out_shape=jax.ShapeDtypeStruct(tiled.shape, jnp.float32),
+        out_shape=pltpu.VMEM(tiled.shape, jnp.float32),
         in_specs=[anywhere, vmem, vmem, vmem],
-        out_specs=anywhere,
+        out_specs=vmem,
         scratch_shapes=[
             pltpu.VMEM((local_channels, tiled.shape[1] + 16, LANES), jnp.float32),
             pltpu.VMEM((devices, tiles, block, LANES), jnp.float32),
@@ -311,7 +305,6 @@
             pltpu.VMEM((devices, local_channels, tiles * local_rows, LANES), jnp.float32),
             pltpu.VMEM((2, devices * block, devices * block), jnp.bfloat16),
             dma((local_channels,)),
-            dma((CHUNKS,)),
             dma((CHUNKS, devices)),
             dma((CHUNKS, devices)),
             dma((CHUNKS, devices)),

time: 33.5 us -> 32.3 us (0.964)
  local copies, waits for them, and re-layouts: 1.87 us -> 0.8 us
    unnamed x1, local copies, waits for them, and re-layouts: 1.87 us -> 0.8 us
where the time goes in v2:
time: 32.3 us; the launch traced here: 32 us
  Pallas kernels  31.2 us (97%)
  local copies, waits for them, and re-layouts  0.8 us (2%)
    pallas_call x1, Pallas kernels, fused(): pl.pallas_call(functools.partial(fused_kernel, chans, bands), out_shape=p...  31.2 us
    unnamed x1, local copies, waits for them, and re-layouts  0.8 us

profile of v2, /device:TPU:0, one launch (start us, length us, event | category | flops | bytes accessed | tf_op | source)
XLA Modules:
  0.0 32.0 jit_solution(3643235551820324355)
XLA Ops:
  0.0 31.2 %shard_map.46 = f32[4,256,128]{2,1,0:T(8,128)S(1)} custom-call(f32[4,256,128]{2,1,0:T(8,128)} %bitcast.11, f32[4,257]{1,0:T(4,128)} %row_taps.1, f32[16,257]{1,0:T(8,128)} %column_taps.1, f32[16,16]{1,0:T(8,128)} %channel_mix.1), custom_call_target="tpu_custom_call" | custom-call | tf_op jit(solution)/shard_map/pallas_call | solution.py:296
  31.2 0.8 %copy.8 = f32[4,4,8192]{2,1,0:T(4,128)} copy(f32[4,4,8192]{2,1,0:T(4,128)S(1)} %bitcast.10) | data formatting | bytes 1048576

commit v3 on v2

--- a/solution.py
+++ b/solution.py
@@ -162,8 +162,8 @@
 
 def fused_kernel(
     chans, bands, x_hbm, row_taps, column_taps, channel_mix, out_ref,
-    x_buf, send_one, recv_one, send_two, mixing,
-    in_sem, send_one_sem, recv_one_sem, send_two_sem, recv_two_sem,
+    x_buf, tables, send_one, recv_one, send_two, mixing,
+    ready, in_sem, send_one_sem, recv_one_sem, send_two_sem, recv_two_sem,
 ):
     local_channels, x_rows, _ = x_hbm.shape
     devices, _, block_rows, _ = send_two.shape
@@ -172,75 +172,131 @@
     chan, band = lax.axis_index("chan"), lax.axis_index("band")
     me = band * chans + chan
 
-    barrier = pltpu.get_barrier_semaphore()
+    half = bands // 2
+    x_half = x_rows // 2
     peers = []
-    for band_step in sorted(range(bands), key=lambda step: (-(2 * step // bands), step)):
+    for band_step in sorted(range(bands), key=lambda step: (step < half, step)):
         for chan_step in range(chans):
             if band_step or chan_step:
-                peers.append((chan ^ chan_step, band ^ band_step))
-    names = [{"chan": to_chan, "band": to_band} for to_chan, to_band in peers]
-    slots = [to_band * chans + to_chan for to_chan, to_band in peers]
-    for name in names:
-        pl.semaphore_signal(barrier, inc=1, device_id=name, device_id_type=pl.DeviceIdType.MESH)
-
+                to_chan, to_band = chan ^ chan_step, band ^ band_step
+                slot = to_band * chans + to_chan
+                name = {"chan": to_chan, "band": to_band}
+                peers.append((name, slot))
+
+    def each_peer(visit, also=None):
+        for name, slot in peers:
+            if also is None:
+                visit(name, slot)
+            else:
+                pl.when(also(slot))(functools.partial(visit, name, slot))
+
+    barrier = pltpu.get_barrier_semaphore()
+    greet = functools.partial(
+        pl.semaphore_signal, inc=1, device_id_type=pl.DeviceIdType.MESH
+    )
+    each_peer(lambda name, slot: greet(barrier, device_id=name), lambda slot: slot > me)
     loads = [
         pltpu.make_async_copy(x_hbm.at[c], x_buf.at[c, pl.ds(8, x_rows)], in_sem.at[c])
         for c in range(local_channels)
     ]
     for load in loads:
         load.start()
+
+    @pl.when(me > 0)
+    def _():
+        pl.semaphore_wait(barrier, me)
+
+    each_peer(lambda name, slot: greet(ready.at[me], device_id=name), lambda slot: slot < me)
+
     edge = jnp.zeros((8, LANES), jnp.float32)
     for c in range(local_channels):
         x_buf[c, 0:8, :] = edge
         x_buf[c, x_rows + 8 : x_rows + 16, :] = edge
-
-    for c in range(local_channels):
-        table = split(filter_table(row_taps[c : c + 1, :]))
-        loads[c].wait()
-        window = jnp.concatenate(
-            [
-                x_buf[c, 8 + (k - 1) * local_rows : 8 + (k - 1) * local_rows + x_rows, :]
-                for k in range(3)
+        tables[c, 0], tables[c, 1] = split(filter_table(row_taps[c : c + 1, :]))
+
+    def filter_half(which, first):
+        start = pl.multiple_of(which * x_half, 8)
+        for c in range(local_channels):
+            if first:
+                loads[c].wait()
+            wide = x_buf[c, pl.ds(start, x_half + 16), :]
+            window = jnp.concatenate(
+                [
+                    wide[8 + (k - 1) * local_rows : 8 + (k - 1) * local_rows + x_half]
+                    for k in range(3)
+                ],
+                axis=1,
+            )
+            filtered = product(split(window), (tables[c, 0], tables[c, 1]), ((1,), (1,)))
+            for device in range(devices // 2):
+                for tile in range(tiles):
+                    at = (device * tiles + tile) * local_rows
+                    send_one[
+                        which * (devices // 2) + device,
+                        tile,
+                        c * local_rows : (c + 1) * local_rows,
+                        :,
+                    ] = filtered[at : at + local_rows, :]
+
+    step = tiles // CHUNKS
+
+    def copy_one(chunk, name, slot):
+        part = pl.ds(chunk * step, step)
+        return pltpu.make_async_remote_copy(
+            src_ref=send_one.at[slot, part],
+            dst_ref=recv_one.at[part, me],
+            send_sem=send_one_sem.at[chunk, slot],
+            recv_sem=recv_one_sem.at[chunk, me],
+            device_id=name,
+            device_id_type=pl.DeviceIdType.MESH,
+        )
+
+    def send_one_to(chunk, name, slot):
+        if chunk == 0:
+
+            @pl.when(slot > me)
+            def _():
+                pl.semaphore_wait(ready.at[slot], 1)
+
+        copy_one(chunk, name, slot).start()
+
+    filter_half(1 - band // half, True)
+    far = half * chans
+    for name, slot in peers[:far]:
+        send_one_to(0, name, slot)
+    filter_half(band // half, False)
+    for name, slot in peers[far:]:
+        send_one_to(0, name, slot)
+    for name, slot in peers:
+        send_one_to(1, name, slot)
+    recv_one[:, me] = send_one[me]
+
+    table = mixing_table(
+        column_taps[...], channel_mix[...], chans, bands, local_channels, local_rows
+    )
+    mixing[0], mixing[1] = split(table)
+
+    rows = step * local_rows
+
+    def copy_two(chunk, name, slot):
+        return pltpu.make_async_remote_copy(
+            src_ref=send_two.at[slot, :, pl.ds(chunk * rows, rows)],
+            dst_ref=out_ref.at[
+                :, pl.ds(pl.multiple_of(me * block_rows + chunk * rows, 8), rows)
             ],
-            axis=1,
+            send_sem=send_two_sem.at[chunk, slot],
+            recv_sem=recv_two_sem.at[chunk, me],
+            device_id=name,
+            device_id_type=pl.DeviceIdType.MESH,
         )
-        filtered = product(split(window), table, ((1,), (1,)))
-        for device in range(devices):
-            for tile in range(tiles):
-                at = (device * tiles + tile) * local_rows
-                send_one[device, tile, c * local_rows : (c + 1) * local_rows, :] = filtered[
-                    at : at + local_rows, :
-                ]
-
-    pl.semaphore_wait(barrier, len(peers))
-    step = tiles // CHUNKS
-    copies = []
+
     for chunk in range(CHUNKS):
         part = pl.ds(chunk * step, step)
-        for name, slot in zip(names, slots):
-            copy = pltpu.make_async_remote_copy(
-                src_ref=send_one.at[slot, part],
-                dst_ref=recv_one.at[part, me],
-                send_sem=send_one_sem.at[chunk, slot],
-                recv_sem=recv_one_sem.at[chunk, me],
-                device_id=name,
-                device_id_type=pl.DeviceIdType.MESH,
-            )
-            copy.start()
-            copies.append(copy)
-    recv_one[:, me] = send_one[me]
-
-    table = mixing_table(
-        column_taps[...], channel_mix[...], chans, bands, local_channels, local_rows
-    )
-    mixing[0], mixing[1] = split(table)
-
-    rows = step * local_rows
-    for chunk in range(CHUNKS):
-        part = pl.ds(chunk * step, step)
-        for slot in slots:
+        def landed_one(name, slot):
             landed = recv_one.at[part, slot]
             pltpu.make_async_copy(landed, landed, recv_one_sem.at[chunk, slot]).wait()
+
+        each_peer(landed_one)
         columns = jnp.concatenate(
             [
                 recv_one[chunk * step + tile].reshape(mixing.shape[1], LANES)
@@ -257,29 +313,20 @@
                     send_two[device, c, to : to + local_rows, :] = mixed[
                         at : at + local_rows, tile * LANES : (tile + 1) * LANES
                     ]
-        here = pl.ds(chunk * rows, rows)
         there = pl.ds(pl.multiple_of(me * block_rows + chunk * rows, 8), rows)
-        for name, slot in zip(names, slots):
-            copy = pltpu.make_async_remote_copy(
-                src_ref=send_two.at[slot, :, here],
-                dst_ref=out_ref.at[:, there],
-                send_sem=send_two_sem.at[chunk, slot],
-                recv_sem=recv_two_sem.at[chunk, me],
-                device_id=name,
-                device_id_type=pl.DeviceIdType.MESH,
-            )
-            copy.start()
-            copies.append(copy)
+        each_peer(lambda name, slot: copy_two(chunk, name, slot).start())
         out_ref[:, there, :] = send_two[me, :, chunk * rows : (chunk + 1) * rows, :]
 
+    def finish(chunk, name, slot):
+        landed = out_ref.at[
+            :, pl.ds(pl.multiple_of(slot * block_rows + chunk * rows, 8), rows)
+        ]
+        pltpu.make_async_copy(landed, landed, recv_two_sem.at[chunk, slot]).wait()
+        copy_one(chunk, name, slot).wait_send()
+        copy_two(chunk, name, slot).wait_send()
+
     for chunk in range(CHUNKS):
-        for slot in slots:
-            landed = out_ref.at[
-                :, pl.ds(pl.multiple_of(slot * block_rows + chunk * rows, 8), rows)
-            ]
-            pltpu.make_async_copy(landed, landed, recv_two_sem.at[chunk, slot]).wait()
-    for copy in copies:
-        copy.wait_send()
+        each_peer(functools.partial(finish, chunk))
 
 
 def fused(chans, bands, slide_region, row_taps, column_taps, channel_mix):
@@ -300,10 +347,12 @@
         out_specs=vmem,
         scratch_shapes=[
             pltpu.VMEM((local_channels, tiled.shape[1] + 16, LANES), jnp.float32),
+            pltpu.VMEM((local_channels, 2, LANES, 3 * LANES), jnp.bfloat16),
             pltpu.VMEM((devices, tiles, block, LANES), jnp.float32),
             pltpu.VMEM((tiles, devices, block, LANES), jnp.float32),
             pltpu.VMEM((devices, local_channels, tiles * local_rows, LANES), jnp.float32),
             pltpu.VMEM((2, devices * block, devices * block), jnp.bfloat16),
+            pltpu.SemaphoreType.REGULAR((devices,)),
             dma((local_channels,)),
             dma((CHUNKS, devices)),
             dma((CHUNKS, devices)),
@@ -327,6 +376,7 @@
     fits = (
         power_of_two(chans)
         and power_of_two(bands)
+        and bands > 1
         and width % (devices * LANES * CHUNKS) == 0
         and margin == LANES
         and column_taps.shape[1] == row_taps.shape[1]

time: 32.3 us -> 32.1 us (level)
  no operation moved by 1% of the time
where the time goes in v3:
time: 32.1 us; the launch traced here: 31.9 us
  Pallas kernels  31 us (97%)
  local copies, waits for them, and re-layouts  0.8 us (2%)
    pallas_call x1, Pallas kernels, fused(): pl.pallas_call(functools.partial(fused_kernel, chans, bands), out_shape=p...  31 us
    unnamed x1, local copies, waits for them, and re-layouts  0.8 us

profile of v3, /device:TPU:0, one launch (start us, length us, event | category | flops | bytes accessed | tf_op | source)
XLA Modules:
  0.0 31.9 jit_solution(11175018947560493434)
XLA Ops:
  0.0 31.0 %shard_map.46 = f32[4,256,128]{2,1,0:T(8,128)S(1)} custom-call(f32[4,256,128]{2,1,0:T(8,128)} %bitcast.11, f32[4,257]{1,0:T(4,128)} %row_taps.1, f32[16,257]{1,0:T(8,128)} %column_taps.1, f32[16,16]{1,0:T(8,128)} %channel_mix.1), custom_call_target="tpu_custom_call" | custom-call | tf_op jit(solution)/shard_map/pallas_call | solution.py:343
  31.1 0.8 %copy.8 = f32[4,4,8192]{2,1,0:T(4,128)} copy(f32[4,4,8192]{2,1,0:T(4,128)S(1)} %bitcast.10) | data formatting | bytes 1048576
